TPU v7x, 512 devices: a whole 4x4x16 slice. The times are simulated.
512 devices in a mesh: frow: 32 (over z_lo, y, core), fcol: 16 (over z_hi, x).
Axes of the slice: x: 4, y: 4, z: 16 (z_hi: 4, z_lo: 4; z = z_hi * 4 + z_lo), core: 2. Of those that a mesh axis runs over, the one named last changes fastest.
Arguments:
- model_image: bfloat16 [16384, 16384], P('frow', 'fcol'), may hold values from -6 to 6
- weight_grids: bfloat16 [8, 256, 256], replicated, may hold values from 0.19921875 to 2
- strip_offsets: int32 [2], replicated, may hold values from 0 to 63
- subgrid_offsets: int32 [2, 32], replicated, may hold values from 0 to 63
- grid_index: int32 [2, 32], replicated, may hold values from 0 to 7
Outputs:
- residual_update: float32 [16384, 16384], P('frow', 'fcol')
Inputs may be any that keep to these rules, and one draw needn't show every extreme that they name: `strip_offsets`: two strips may coincide. `subgrid_offsets`: two subgrids of one strip may coincide.
All inputs are finite; a program needn't handle non-finite values.
Results may differ from a plain program's by a relative error of at most 0.03.
Values may be sent and summed in bfloat16 or wider, within the bound.
No kernel may reach another device: no remote copies, remote signals or barrier semaphores. Data moves between devices by JAX's collectives and lax.ppermute only.
A program may use at most 64 MiB of HBM per device.

v0:
```python
import math
import jax
import jax.numpy as jnp
import numpy as np
from jax import lax
from jax.sharding import Mesh
from jax.sharding import PartitionSpec as P

F32 = jnp.float32
BF16 = jnp.bfloat16
STRIP = 256
SUB = 256
AXES = ("zl", "y", "core", "zh", "x")
NEAR = ("zl", "y", "x")


def turn(numerator, denominator):
    angle = (numerator % denominator).astype(F32) * (2.0 * math.pi / denominator)
    return (jnp.cos(angle), jnp.sin(angle))


def tables(quads, blocks, sub_cols, uv_cols):
    r = np.arange(STRIP).reshape(quads, 1, -1, 1, 1)
    p = np.arange(2).reshape(1, 2, 1, 1, 1)
    q = np.arange(2).reshape(1, 1, 1, 2, 1)
    b = np.arange(STRIP).reshape(1, 1, 1, 1, -1)
    phase = 2.0 * np.pi * (r * b % STRIP) / STRIP + (p - q) * (np.pi / 2)
    phase = phase.reshape(2 * STRIP, 2 * STRIP)
    rows = (np.cos(phase), -np.sin(phase))
    d = np.arange(SUB)
    phase = 2.0 * np.pi * (np.outer(d, d) % SUB) / SUB
    cos, sin = (np.cos(phase), np.sin(phase))
    cols = np.block([[cos, -sin], [sin, cos]])
    u = np.arange(uv_cols).reshape(1, -1, 1, 1, 1)
    p = np.arange(2).reshape(2, 1, 1, 1, 1)
    c = blocks.reshape(1, 1, -1, 1, 1)
    q = np.arange(2).reshape(1, 1, 1, 2, 1)
    phase = 2.0 * np.pi * (u * c % uv_cols) / uv_cols + (p - q) * (np.pi / 2)
    phase = np.broadcast_to(np.cos(phase), (2, uv_cols, blocks.size, 2, sub_cols))
    return (rows, cols, phase.reshape(2, uv_cols, -1))


def body(model_image, weight_grids, strip_offsets, subgrid_offsets, grid_index):
    rows_local, facet_width = model_image.shape
    ny, nx, nzl, nzh = (lax.axis_size(a) for a in ("y", "x", "zl", "zh"))
    ncore = lax.axis_size("core")
    zl, y, core, zh, x = (lax.axis_index(a) for a in AXES)
    width = facet_width // ny
    modulus = facet_width * nx * nzh
    uv_cols = modulus // SUB
    periods = rows_local // STRIP
    quads = nzl * ny * nx
    rows_each = STRIP // quads
    count = subgrid_offsets.shape[1]
    strips = strip_offsets.shape[0]
    order = np.arange(uv_cols).reshape(nzh, nx, ny).transpose(0, 2, 1).reshape(-1)
    (rows_cos, rows_sin), cols_table, block_table = tables(quads, order, rows_each, uv_cols)
    own, other = (core, 1 - core)
    offset_own = lax.dynamic_index_in_dim(strip_offsets, own, 0, keepdims=False)
    offset_other = lax.dynamic_index_in_dim(strip_offsets, other, 0, keepdims=False)
    span = (zl * ny + jnp.arange(ny, dtype=jnp.int32)) * ncore + core
    span = span[:, None] * periods + jnp.arange(periods, dtype=jnp.int32)
    own_cos, own_sin = turn(offset_own * span, uv_cols)
    other_cos, other_sin = turn(offset_other * span, uv_cols)
    cos_b, sin_b = turn(offset_own * jnp.arange(STRIP, dtype=jnp.int32), modulus)
    cos_b = jnp.concatenate([cos_b, cos_b])[None]
    sin_b = jnp.concatenate([sin_b, sin_b])[None]
    row_phases = (
        jnp.asarray(rows_cos, BF16).astype(F32) * cos_b
        + jnp.asarray(rows_sin, BF16).astype(F32) * sin_b
    ).astype(BF16)
    gathered = lax.all_to_all(model_image, "y", 1, 0, tiled=True)
    pixels = gathered.reshape(ny, periods, STRIP, width).astype(F32)

    def fold(cos, sin):
        real = jnp.sum(pixels * cos[:, :, None, None], axis=(0, 1))
        imag = -jnp.sum(pixels * sin[:, :, None, None], axis=(0, 1))
        return jnp.concatenate([real, imag], axis=0)

    swap = [(0, 1), (1, 0)]
    received = lax.ppermute(fold(other_cos, other_sin).astype(BF16), "core", swap)
    folded = (fold(own_cos, own_sin) + received.astype(F32)).astype(BF16)
    partial = jnp.dot(row_phases, folded, preferred_element_type=F32).astype(BF16)
    parts = lax.all_to_all(partial.reshape(quads, 2 * rows_each, width), NEAR, 0, 0, tiled=True)
    parts = parts.reshape(nzl, ny * nx, 2 * rows_each, width).astype(F32)
    strip = jnp.sum(parts, axis=0).astype(BF16).reshape(ny * nx * 2 * rows_each, width)
    whole = lax.all_gather(strip, "zh", axis=0, tiled=True)
    quad = (zl * ny + y) * nx + x
    shifts = lax.dynamic_index_in_dim(subgrid_offsets, own, 0, keepdims=False)
    chosen = lax.dynamic_index_in_dim(grid_index, own, 0, keepdims=False)
    lines = rows_each * count
    line_shift = jnp.tile(shifts, rows_each)
    line_row = jnp.repeat(jnp.arange(rows_each, dtype=jnp.int32), count)
    pick = (line_shift[:, None] == jnp.arange(uv_cols, dtype=jnp.int32)[None]).astype(BF16)
    table_row = jnp.arange(2 * uv_cols * rows_each, dtype=jnp.int32) % rows_each
    same = line_row[:, None] == table_row[None]
    spread = [
        jnp.where(
            same,
            jnp.dot(pick, jnp.asarray(block_table[part], BF16), preferred_element_type=F32),
            0.0,
        )
        for part in range(2)
    ]
    spread = jnp.concatenate(spread, axis=0).astype(BF16)
    cos_d, sin_d = turn(shifts[:, None] * jnp.arange(SUB, dtype=jnp.int32)[None], modulus)
    cos_d = jnp.tile(cos_d, (rows_each, 1))
    sin_d = jnp.tile(sin_d, (rows_each, 1))
    fourier = jnp.asarray(cols_table, BF16)
    mixed = jnp.dot(spread, whole, preferred_element_type=F32)
    real, imag = (mixed[:lines], mixed[lines:])
    turned = jnp.concatenate(
        [real * cos_d + imag * sin_d, imag * cos_d - real * sin_d], axis=1
    ).astype(BF16)
    spectra = jnp.dot(turned, fourier, preferred_element_type=F32)
    grid_rows = lax.dynamic_slice_in_dim(weight_grids, quad * rows_each, rows_each, 1)
    grids = grid_rows.shape[0]
    line_grid = jnp.tile(chosen, rows_each)[:, None] * rows_each + line_row[:, None]
    select = (line_grid == jnp.arange(grids * rows_each, dtype=jnp.int32)[None]).astype(BF16)
    weights = jnp.dot(select, grid_rows.reshape(grids * rows_each, SUB), preferred_element_type=F32)
    weighted = (spectra * jnp.concatenate([weights, weights], axis=1)).astype(BF16)
    returned = lax.dot_general(
        weighted, fourier, (((1,), (1,)), ((), ())), preferred_element_type=F32
    )
    real, imag = (returned[:, :SUB], returned[:, SUB:])
    turned = jnp.concatenate(
        [real * cos_d - imag * sin_d, imag * cos_d + real * sin_d], axis=0
    ).astype(BF16)
    held = strip.shape[0]
    mine = lax.dynamic_slice_in_dim(spread, zh * held, held, 1)
    back = lax.dot_general(mine, turned, (((0,), (0,)), ((), ())), preferred_element_type=F32)
    back = back.astype(BF16).reshape(ny * nx, 2 * rows_each, width)
    back = jnp.tile(back, (nzl, 1, 1))
    image = lax.all_to_all(back, NEAR, 0, 0, tiled=True).reshape(2 * STRIP, width)
    scale = 1.0 / (modulus * math.sqrt(count * SUB) * math.sqrt(strips * STRIP))
    expanded = lax.dot_general(
        row_phases, image, (((0,), (0,)), ((), ())), preferred_element_type=F32
    )
    expanded = (expanded * scale).astype(BF16)
    received = lax.ppermute(expanded, "core", swap)

    def unfold(value, cos, sin):
        value = value.astype(F32)[None, None]
        real, imag = (value[:, :, :STRIP], value[:, :, STRIP:])
        return real * cos[:, :, None, None] - imag * sin[:, :, None, None]

    update = unfold(expanded, own_cos, own_sin) + unfold(received, other_cos, other_sin)
    update = update.astype(BF16).reshape(ny * rows_local, width)
    return lax.all_to_all(update, "y", 0, 1, tiled=True).astype(F32)


def solution(mesh):
    shape = {"zl": 4, "y": 4, "core": 2, "zh": 4, "x": 4}
    finer = Mesh(mesh.devices.reshape(tuple(shape.values())), tuple(shape))
    rows, cols = (("zl", "y", "core"), ("zh", "x"))
    return jax.shard_map(
        body,
        mesh=finer,
        in_specs=(P(rows, cols), P(), P(), P(), P()),
        out_specs=P(rows, cols),
        check_vma=False,
    )
```

profile of v0, /device:TPU:1, one launch (start us, length us, event | category | flops | bytes accessed | tf_op | source)
XLA Modules:
  0.0 139.9 jit_solution(11549442983529142427)
XLA Ops:
  0.0 0.0 copy-start
  0.0 1.6 %copy.15 = bf16[512,1024]{0,1:T(8,128)(2,1)S(1)} copy(bf16[512,1024]{1,0:T(8,128)(2,1)} %param.10) | data formatting | bytes 2097152 | tf_op args[0]
  1.6 0.0 copy-start.9
  1.6 1.3 copy.16
  2.9 5.0 %all-to-all-start = ((bf16[512,4,256]{2,0,1:T(8,128)(2,1)}), bf16[512,4,256]{2,0,1:T(8,128)(2,1)S(1)}, u32[]{:S(2)}, u32[]{:S(2)}) async-start(bf16[512,4,256]{2,0,1:T(8,128)(2,1)} %copy.16), calls=%async_computation | async-start | bytes 2097152 | tf_op jit(solution)/shard_map/all_to_all | solution.py:72
  7.9 0.0 copy-done.9
  7.9 0.7 fusion.74
  8.6 1.4 fusion.64
  10.0 0.1 broadcast_bitcast_fusion.2
  10.1 0.1 broadcast_bitcast_fusion
  10.2 0.0 copy-start.5
  10.2 1.2 fusion.68
  11.4 6.3 %all-to-all-done = bf16[512,4,256]{2,0,1:T(8,128)(2,1)S(1)} async-done(((bf16[512,4,256]{2,0,1:T(8,128)(2,1)}), bf16[512,4,256]{2,0,1:T(8,128)(2,1)S(1)}, u32[]{:S(2)}, u32[]{:S(2)}) %all-to-all-start) | async-done | bytes 1048608 | tf_op jit(solution)/shard_map/all_to_all | solution.py:72
  17.7 2.5 %fusion.2 = (f32[512,256]{1,0:T(8,128)S(1)}, f32[512,256]{1,0:T(8,128)}, f32[512,256]{1,0:T(8,128)}, f32[512,256]{1,0:T(8,128)}) fusion(bf16[512,4,256]{2,0,1:T(8,128)(2,1)S(1)} %all-to-all-done, f32[4,512]{1,0:T(4,128)S(1)} %bitcast.131, f32[4,512]{1,0:T(4,128)S(1)} %bitcast.129, f32[4,512]{1,0:T(4,128)S(1)} %bitcast.125, f32[4,512]{1,0:T(4,128)S(1)} %bitcast.127), kind=kLoop, calls=%fused_computation.6 | loop fusion | flops 4194304 | bytes 3178496 | tf_op jit(solution)/shard_map/reduce_sum | solution.py:76
  20.2 0.0 copy-done.3
  20.2 0.0 copy-done.5
  20.2 0.0 copy-start.1
  20.2 0.0 copy-start.2
  20.3 1.2 reduce_sum.87
  21.5 0.7 pad_maximum_fusion.2
  22.2 8.4 %collective-permute-start = (bf16[512,256]{1,0:T(8,128)(2,1)}, bf16[512,256]{1,0:T(8,128)(2,1)}, u32[]{:S(2)}, u32[]{:S(2)}) collective-permute-start(bf16[512,256]{1,0:T(8,128)(2,1)} %pad_maximum_fusion.2), channel_id=1, source_target_pairs={{0,16},{16,0},{1,17},{17,1},{2,18},{18,2},{3,19},{19,3},{4,20},{20... | collective-permute-start | bytes 786440 | tf_op jit(solution)/shard_map/ppermute | solution.py:81
  30.6 0.7 pad_maximum_fusion.4
  31.4 0.7 pad_maximum_fusion.3
  32.1 1.8 %reduce_sum.81 = f32[256,256]{1,0:T(8,128)} reduce(f32[2,256,256]{2,1,0:T(8,128)} %bitcast.115, f32[]{:T(128)} %constant.111.clone.1), dimensions={0}, to_apply=%region_3.4 | reduce | flops 65536 | bytes 786436 | tf_op jit(solution)/shard_map/reduce_sum | solution.py:77
  33.9 1.1 reduce_sum.62
  35.1 0.0 copy-start.11
  35.1 0.0 copy-start.12
  35.1 1.0 neg.6
  36.1 0.0 collective-permute-done
  36.1 2.0 %fusion.5 = bf16[64,8,256]{2,1,0:T(8,128)(2,1)} fusion(f32[512,512]{1,0:T(8,128)S(1)} %copy-done.1, f32[512,512]{1,0:T(8,128)S(1)} %copy-done.2, f32[512]{0:T(512)S(1)} %pad_maximum_fusion.4, f32[512]{0:T(512)S(1)} %pad_maximum_fusion.3, f32[256,256]{1,0:T(8,128)S(1)} %neg.6, f32[256,256]{1,0:T(8,128)S(1)} %reduce_sum.62, ...), kind=kOutput, calls=%fused_computation.12 | convolution fusion | flops 135921664 | bytes 3149824 | tf_op jit(solution)/shard_map/dot_general | solution.py:83
  38.1 9.5 %all-to-all-start.1 = ((bf16[64,8,256]{2,1,0:T(8,128)(2,1)}), bf16[64,8,256]{2,1,0:T(8,128)(2,1)S(1)}, u32[]{:S(2)}, u32[]{:S(2)}) async-start(bf16[64,8,256]{2,1,0:T(8,128)(2,1)} %fusion.5), calls=%async_computation.1 | async-start | bytes 524288 | tf_op jit(solution)/shard_map/all_to_all | solution.py:84
  47.6 0.0 copy-done.11
  47.6 0.0 copy-done.12
  47.7 0.1 mul.360
  47.8 0.6 eq.66
  48.4 0.1 eq.62
  48.5 0.6 reshape.281
  49.1 0.0 copy-done.10
  49.1 0.8 fusion.47
  49.9 0.9 fusion.36
  50.9 1.7 %fusion.8 = bf16[128,512]{1,0:T(8,128)(2,1)} fusion(bf16[64,512]{1,0:T(8,128)(2,1)} %constant.128.clone, s32[512]{0:T(512)S(1)} %add_select_fusion.3, s32[128]{0:T(128)} %copy-done.10, s32[128]{0:T(128)} %eq.66), kind=kOutput, calls=%fused_computation.18 | convolution fusion | flops 8593408 | bytes 199680 | tf_op jit(solution)/shard_map/dot_general | solution.py:100
  52.6 1.7 %fusion.7 = bf16[128,512]{1,0:T(8,128)(2,1)} fusion(bf16[64,512]{1,0:T(8,128)(2,1)} %constant.127.clone, s32[512]{0:T(512)S(1)} %add_select_fusion.3, s32[128]{0:T(128)} %copy-done.10, s32[128]{0:T(128)} %eq.66), kind=kOutput, calls=%fused_computation.17 | convolution fusion | flops 8593408 | bytes 199680 | tf_op jit(solution)/shard_map/dot_general | solution.py:100
  54.3 5.2 %all-to-all-done.1 = bf16[64,8,256]{2,1,0:T(8,128)(2,1)S(1)} async-done(((bf16[64,8,256]{2,1,0:T(8,128)(2,1)}), bf16[64,8,256]{2,1,0:T(8,128)(2,1)S(1)}, u32[]{:S(2)}, u32[]{:S(2)}) %all-to-all-start.1) | async-done | bytes 262176 | tf_op jit(solution)/shard_map/all_to_all | solution.py:84
  59.5 0.7 reduce_sum.88
  60.2 22.4 %all_gather.3 = bf16[512,256]{1,0:T(8,128)(2,1)S(1)} all-gather(bf16[128,256]{1,0:T(8,128)(2,1)} %bitcast.124), channel_id=1, replica_groups=mesh['zl'=4,'y'=4,'core'=2,'zh'=4,'x'=4] {'zh'}, dimensions={0}, use_global_device_ids=true | all-gather | bytes 327680 | tf_op jit(solution)/shard_map/all_gather | solution.py:87
  82.5 1.2 fusion.17
  83.8 1.4 %fusion.26 = (bf16[128,256]{1,0:T(8,128)(2,1)}, bf16[128,256]{1,0:T(8,128)(2,1)S(1)}) fusion(f32[256,256]{1,0:T(8,128)S(1)} %fusion.17, f32[32,256]{1,0:T(8,128)} %get-tuple-element.18, f32[32,256]{1,0:T(8,128)} %get-tuple-element.17), kind=kLoop, calls=%fused_computation.57 | loop fusion | flops 262144 | bytes 458752 | tf_op jit(solution)/shard_map/convert.9
  85.2 1.8 %fusion.75 = f32[128,512]{1,0:T(8,128)} fusion(bf16[128,256]{1,0:T(8,128)(2,1)S(1)} %get-tuple-element.16, bf16[256,512]{1,0:T(8,128)(2,1)} %constant.132), kind=kOutput, calls=%fused_computation.132 | convolution fusion | flops 33554432 | bytes 589824 | tf_op jit(solution)/shard_map/dot_general | solution.py:115
  87.0 1.6 %fusion.10 = f32[128,512]{1,0:T(8,128)S(1)} fusion(bf16[512,512]{1,0:T(8,128)(2,1)} %constant.129.clone, f32[128,512]{1,0:T(8,128)} %fusion.75, bf16[128,256]{1,0:T(8,128)(2,1)} %get-tuple-element.15, bf16[256,512]{1,0:T(8,128)(2,1)} %constant.133, f32[128,256]{1,0:T(8,128)S(1)} %fusion.36), kind=kOutput, calls=%fused_computation.20 | convolution fusion | flops 100925440 | bytes 1507328 | tf_op jit(solution)/shard_map/dot_general | solution.py:122
  88.7 0.8 fusion.28
  89.5 1.0 fusion.11
  90.5 17.1 %all_to_all.33 = bf16[64,8,256]{2,1,0:T(8,128)(2,1)S(1)} all-to-all(bf16[64,8,256]{2,1,0:T(8,128)(2,1)S(1)} %bitcast.123), channel_id=1, replica_groups=mesh['zl'=4,'y'=4,'core'=2,'zh'=4,'x'=4] {'zl','y','x'}, dimensions={0} | all-to-all | bytes 524288 | tf_op jit(solution)/shard_map/all_to_all | solution.py:134
  107.5 1.1 bitcast_convert_fusion.1
  108.7 6.2 %collective-permute-start.1 = (bf16[512,256]{1,0:T(8,128)(2,1)S(1)}, bf16[512,256]{1,0:T(8,128)(2,1)S(1)}, u32[]{:S(2)}, u32[]{:S(2)}) collective-permute-start(bf16[512,256]{1,0:T(8,128)(2,1)S(1)} %get-tuple-element.26), channel_id=1, source_target_pairs={{0,16},{16,0},{1,17},{17,1},{2,18},{18,2},{3,19},{19,3},{4,20},{20... | collective-permute-start | bytes 786440 | tf_op jit(solution)/shard_map/ppermute | solution.py:140
  114.9 1.1 collective-permute-done.1
  116.1 0.0 copy-start.4
  116.1 0.0 copy-start.6
  116.3 0.5 copy-done.4
  116.8 0.0 copy-done.6
  116.8 1.2 add_convert_fusion
  118.0 17.2 %all_to_all.34 = bf16[4,512,256]{2,1,0:T(8,128)(2,1)S(1)} all-to-all(bf16[4,512,256]{2,1,0:T(8,128)(2,1)S(1)} %add_convert_fusion), channel_id=1, replica_groups=mesh['zl'=4,'y'=4,'core'=2,'zh'=4,'x'=4] {'y'}, dimensions={0} | all-to-all | bytes 2097152 | tf_op jit(solution)/shard_map/all_to_all | solution.py:149
  135.3 1.3 copy.17
  136.6 1.5 %convert_element_type.115 = f32[4,512,256]{1,2,0:T(8,128)S(1)} convert(bf16[4,512,256]{1,2,0:T(8,128)(2,1)} %copy.17) | non-fusion elementwise | flops 524288 | bytes 3145728 | tf_op jit(solution)/shard_map/convert_element_type | solution.py:149
  138.1 1.8 %copy.18 = f32[512,1024]{1,0:T(8,128)} copy(f32[512,1024]{0,1:T(8,128)S(1)} %bitcast.112) | data formatting | bytes 4194304 | tf_op jit(solution)/shard_map/convert_element_type | solution.py:149
  (31 shorter events, 0.4 us)
Async XLA Ops:
  0.0 32.1 %copy-start = (bf16[8,256,256]{2,1,0:T(8,128)(2,1)S(1)}, bf16[8,256,256]{2,1,0:T(8,128)(2,1)}, u32[]{:S(2)}) copy-start(bf16[8,256,256]{2,1,0:T(8,128)(2,1)} %param.11) | copy-start | bytes 3145732
  1.6 6.3 %copy-start.9 = (s32[2]{0:T(128)S(1)}, s32[2]{0:T(128)}, u32[]{:S(2)}) copy-start(s32[2]{0:T(128)} %param.12) | copy-start | bytes 28
  2.9 14.8 %all-to-all-start = ((bf16[512,4,256]{2,0,1:T(8,128)(2,1)}), bf16[512,4,256]{2,0,1:T(8,128)(2,1)S(1)}, u32[]{:S(2)}, u32[]{:S(2)}) async-start(bf16[512,4,256]{2,0,1:T(8,128)(2,1)} %copy.16), calls=%async_computation | async-start | bytes 2097152 | tf_op jit(solution)/shard_map/all_to_all | solution.py:72
  10.1 10.0 %copy-start.3 = (f32[1,4,2,256]{3,1,2,0:T(4,128)}, f32[1,4,2,256]{3,1,2,0:T(4,128)S(1)}, u32[]{:S(2)}) copy-start(f32[1,4,2,256]{3,1,2,0:T(4,128)S(1)} %copy.22) | copy-start | bytes 24580
  10.2 10.0 %copy-start.5 = (f32[1,4,2,256]{3,1,2,0:T(4,128)}, f32[1,4,2,256]{3,1,2,0:T(4,128)S(1)}, u32[]{:S(2)}) copy-start(f32[1,4,2,256]{3,1,2,0:T(4,128)S(1)} %copy.21) | copy-start | bytes 24580
  20.2 15.8 %copy-start.1 = (f32[512,512]{1,0:T(8,128)S(1)}, f32[512,512]{1,0:T(8,128)}, u32[]{:S(2)}) copy-start(f32[512,512]{1,0:T(8,128)} %constant.131) | copy-start | bytes 3145732
  20.2 15.8 %copy-start.2 = (f32[512,512]{1,0:T(8,128)S(1)}, f32[512,512]{1,0:T(8,128)}, u32[]{:S(2)}) copy-start(f32[512,512]{1,0:T(8,128)} %constant.130) | copy-start | bytes 3145732
  22.2 13.8 %collective-permute-start = (bf16[512,256]{1,0:T(8,128)(2,1)}, bf16[512,256]{1,0:T(8,128)(2,1)}, u32[]{:S(2)}, u32[]{:S(2)}) collective-permute-start(bf16[512,256]{1,0:T(8,128)(2,1)} %pad_maximum_fusion.2), channel_id=1, source_target_pairs={{0,16},{16,0},{1,17},{17,1},{2,18},{18,2},{3,19},{19,3},{4,20},{20... | collective-permute-start | bytes 786440 | tf_op jit(solution)/shard_map/ppermute | solution.py:81
  31.4 6.7 %copy-start.7 = (f32[512]{0:T(512)}, f32[512]{0:T(512)S(1)}, u32[]{:S(2)}) copy-start(f32[512]{0:T(512)S(1)} %pad_maximum_fusion.4) | copy-start | bytes 6148
  32.1 6.0 %copy-start.8 = (f32[512]{0:T(512)}, f32[512]{0:T(512)S(1)}, u32[]{:S(2)}) copy-start(f32[512]{0:T(512)S(1)} %pad_maximum_fusion.3) | copy-start | bytes 6148
  35.1 12.6 %copy-start.11 = (s32[2,32]{1,0:T(2,128)S(1)}, s32[2,32]{1,0:T(2,128)}, u32[]{:S(2)}) copy-start(s32[2,32]{1,0:T(2,128)} %param.13) | copy-start | bytes 772
  35.1 12.6 %copy-start.12 = (s32[2,32]{1,0:T(2,128)S(1)}, s32[2,32]{1,0:T(2,128)}, u32[]{:S(2)}) copy-start(s32[2,32]{1,0:T(2,128)} %param.14) | copy-start | bytes 772
  38.1 21.4 %all-to-all-start.1 = ((bf16[64,8,256]{2,1,0:T(8,128)(2,1)}), bf16[64,8,256]{2,1,0:T(8,128)(2,1)S(1)}, u32[]{:S(2)}, u32[]{:S(2)}) async-start(bf16[64,8,256]{2,1,0:T(8,128)(2,1)} %fusion.5), calls=%async_computation.1 | async-start | bytes 524288 | tf_op jit(solution)/shard_map/all_to_all | solution.py:84
  48.5 0.6 copy-start.10
  108.7 7.4 %collective-permute-start.1 = (bf16[512,256]{1,0:T(8,128)(2,1)S(1)}, bf16[512,256]{1,0:T(8,128)(2,1)S(1)}, u32[]{:S(2)}, u32[]{:S(2)}) collective-permute-start(bf16[512,256]{1,0:T(8,128)(2,1)S(1)} %get-tuple-element.26), channel_id=1, source_target_pairs={{0,16},{16,0},{1,17},{17,1},{2,18},{18,2},{3,19},{19,3},{4,20},{20... | collective-permute-start | bytes 786440 | tf_op jit(solution)/shard_map/ppermute | solution.py:140
  116.1 0.7 copy-start.4
  116.1 0.7 copy-start.6
where the time goes:
time: 141 us; the launch traced here: 140 us
  blocking collectives  56.7 us (40%)
  starting transfers between devices  29.1 us (21%)
  other arithmetic  19 us (13%)
  matrix products  13.1 us (9%)
  waiting for transfers between devices  12.6 us (9%)
  local copies, waits for them, and re-layouts  9.07 us (6%)
    all_gather x1, blocking collectives, body(): whole = lax.all_gather(strip, 'zh', axis=0, tiled=True)  22.4 us
    all_to_all x1, blocking collectives, body(): return lax.all_to_all(update, 'y', 0, 1, tiled=True).astype(F32)  17.2 us
    all_to_all x1, blocking collectives, body(): lax.all_to_all(back, NEAR, 0, 0, tiled=True).reshape(2 * STRIP, width)  17.1 us
    all_to_all x1, starting transfers between devices, body(): lax.all_to_all(partial.reshape(quads, 2 * rows_each, width), NEAR, 0, 0,...  9.53 us
    ppermute x1, starting transfers between devices, body(): lax.ppermute(fold(other_cos, other_sin).astype(BF16), 'core', swap)  8.36 us
    all_to_all x1, waiting for transfers between devices, body(): gathered = lax.all_to_all(model_image, 'y', 1, 0, tiled=True)  6.31 us
    ppermute x1, starting transfers between devices, body(): received = lax.ppermute(expanded, 'core', swap)  6.21 us
    all_to_all x1, waiting for transfers between devices, body(): lax.all_to_all(partial.reshape(quads, 2 * rows_each, width), NEAR, 0, 0,...  5.2 us
  transfers between devices with their start and end apart: 4, of which 3 were waited for; matrix products, arithmetic and copies ran while one was open for 11% of the time, Pallas kernels for 0%

commit v1 on v0

--- a/solution.py
+++ b/solution.py
@@ -84,7 +84,9 @@
     parts = lax.all_to_all(partial.reshape(quads, 2 * rows_each, width), NEAR, 0, 0, tiled=True)
     parts = parts.reshape(nzl, ny * nx, 2 * rows_each, width).astype(F32)
     strip = jnp.sum(parts, axis=0).astype(BF16).reshape(ny * nx * 2 * rows_each, width)
-    whole = lax.all_gather(strip, "zh", axis=0, tiled=True)
+    whole = jnp.concatenate(
+        lax.all_to_all(jnp.stack([strip] * lax.axis_size("zh")), "zh", 0, 0), axis=0
+    )
     quad = (zl * ny + y) * nx + x
     shifts = lax.dynamic_index_in_dim(subgrid_offsets, own, 0, keepdims=False)
     chosen = lax.dynamic_index_in_dim(grid_index, own, 0, keepdims=False)

time: 141 us -> 149 us (1.057)
  blocking collectives: 56.7 us -> 34.4 us
  waiting for transfers between devices: 12.6 us -> 29.2 us
  starting transfers between devices: 29.1 us -> 42.3 us
    all_gather x1 -> x0, blocking collectives: 22.4 us -> none  [body(): whole = lax.all_gather(strip, 'zh', axis=0, tiled=True)]
    all_to_all x0 -> x1, starting transfers between devices: none -> 12.1 us  [body(): lax.all_to_all(jnp.stack([strip] * lax.axis_size('zh')), 'zh', 0, 0)]
    all_to_all x0 -> x1, waiting for transfers between devices: none -> 11.6 us  [body(): lax.all_to_all(jnp.stack([strip] * lax.axis_size('zh')), 'zh', 0, 0)]
    all_to_all x1, waiting for transfers between devices: 5.2 us -> 8.96 us  [body(): lax.all_to_all(partial.reshape(quads, 2 * rows_each, width), NEAR, 0, 0,...]
  transfers between devices with their start and end apart: 4 -> 5, of which waited for: 3 -> 4; matrix products, arithmetic and copies ran while one was open for 11% -> 10% of each run, Pallas kernels for 0% -> 0%
where the time goes in v1:
time: 149 us; the launch traced here: 147 us
  starting transfers between devices  42.3 us (28%)
  blocking collectives  34.4 us (23%)
  waiting for transfers between devices  29.2 us (20%)
  other arithmetic  18.2 us (12%)
  matrix products  13.1 us (9%)
  local copies, waits for them, and re-layouts  9.73 us (7%)
    all_to_all x1, blocking collectives, body(): return lax.all_to_all(update, 'y', 0, 1, tiled=True).astype(F32)  17.2 us
    all_to_all x1, blocking collectives, body(): lax.all_to_all(back, NEAR, 0, 0, tiled=True).reshape(2 * STRIP, width)  17.1 us
    all_to_all x1, starting transfers between devices, body(): lax.all_to_all(jnp.stack([strip] * lax.axis_size('zh')), 'zh', 0, 0)  12.1 us
    all_to_all x1, waiting for transfers between devices, body(): lax.all_to_all(jnp.stack([strip] * lax.axis_size('zh')), 'zh', 0, 0)  11.6 us
    all_to_all x1, starting transfers between devices, body(): lax.all_to_all(partial.reshape(quads, 2 * rows_each, width), NEAR, 0, 0,...  9.52 us
    all_to_all x1, waiting for transfers between devices, body(): lax.all_to_all(partial.reshape(quads, 2 * rows_each, width), NEAR, 0, 0,...  8.96 us
    ppermute x1, starting transfers between devices, body(): lax.ppermute(fold(other_cos, other_sin).astype(BF16), 'core', swap)  8.36 us
    all_to_all x1, waiting for transfers between devices, body(): gathered = lax.all_to_all(model_image, 'y', 1, 0, tiled=True)  7.54 us
  transfers between devices with their start and end apart: 5, of which 4 were waited for; matrix products, arithmetic and copies ran while one was open for 10% of the time, Pallas kernels for 0%

profile of v1, /device:TPU:1, one launch (start us, length us, event | category | flops | bytes accessed | tf_op | source)
XLA Modules:
  0.0 147.4 jit_solution(15382442426206237939)
XLA Ops:
  0.0 0.0 copy-start
  0.0 1.6 %copy.15 = bf16[512,1024]{0,1:T(8,128)(2,1)S(1)} copy(bf16[512,1024]{1,0:T(8,128)(2,1)} %param.10) | data formatting | bytes 2097152 | tf_op args[0]
  1.6 0.0 copy-start.9
  1.6 1.3 copy.16
  2.9 5.0 %all-to-all-start = ((bf16[512,4,256]{2,0,1:T(8,128)(2,1)}), bf16[512,4,256]{2,0,1:T(8,128)(2,1)S(1)}, u32[]{:S(2)}, u32[]{:S(2)}) async-start(bf16[512,4,256]{2,0,1:T(8,128)(2,1)} %copy.16), calls=%async_computation | async-start | bytes 2097152 | tf_op jit(solution)/shard_map/all_to_all | solution.py:72
  7.9 0.0 copy-done.9
  7.9 0.7 fusion.74
  8.6 1.4 fusion.64
  9.9 0.1 broadcast_bitcast_fusion.2
  10.0 0.1 broadcast_bitcast_fusion
  10.1 0.0 copy-start.5
  10.1 7.5 %all-to-all-done = bf16[512,4,256]{2,0,1:T(8,128)(2,1)S(1)} async-done(((bf16[512,4,256]{2,0,1:T(8,128)(2,1)}), bf16[512,4,256]{2,0,1:T(8,128)(2,1)S(1)}, u32[]{:S(2)}, u32[]{:S(2)}) %all-to-all-start) | async-done | bytes 1048608 | tf_op jit(solution)/shard_map/all_to_all | solution.py:72
  17.7 2.7 %fusion.2 = (f32[512,256]{1,0:T(8,128)}, f32[512,256]{1,0:T(8,128)}, f32[512,256]{1,0:T(8,128)}, f32[512,256]{1,0:T(8,128)}) fusion(bf16[512,4,256]{2,0,1:T(8,128)(2,1)S(1)} %all-to-all-done, f32[4,512]{1,0:T(4,128)S(1)} %bitcast.133, f32[4,512]{1,0:T(4,128)S(1)} %bitcast.131, f32[4,512]{1,0:T(4,128)S(1)} %bitcast.127, f32[4,512]{1,0:T(4,128)S(1)} %bitcast.129), kind=kLoop, calls=%fused_computation.6 | loop fusion | flops 4194304 | bytes 3178496 | tf_op jit(solution)/shard_map/reduce_sum | solution.py:76
  20.4 0.0 copy-done.3
  20.4 1.2 reduce_sum.84
  21.6 1.1 reduce_sum.87
  22.7 0.7 pad_maximum_fusion.2
  23.5 8.4 %collective-permute-start = (bf16[512,256]{1,0:T(8,128)(2,1)}, bf16[512,256]{1,0:T(8,128)(2,1)}, u32[]{:S(2)}, u32[]{:S(2)}) collective-permute-start(bf16[512,256]{1,0:T(8,128)(2,1)} %pad_maximum_fusion.2), channel_id=1, source_target_pairs={{0,16},{16,0},{1,17},{17,1},{2,18},{18,2},{3,19},{19,3},{4,20},{20... | collective-permute-start | bytes 786440 | tf_op jit(solution)/shard_map/ppermute | solution.py:81
  31.8 0.7 fusion.68
  32.6 0.0 copy-start.8
  32.6 1.8 %reduce_sum.81 = f32[256,256]{1,0:T(8,128)} reduce(f32[2,256,256]{2,1,0:T(8,128)} %bitcast.116, f32[]{:T(128)} %constant.111.clone.1), dimensions={0}, to_apply=%region_3.4 | reduce | flops 65536 | bytes 786436 | tf_op jit(solution)/shard_map/reduce_sum | solution.py:77
  34.4 1.1 reduce_sum.62
  35.5 0.0 copy-start.11
  35.5 0.0 copy-start.12
  35.5 1.0 neg.6
  36.5 0.0 collective-permute-done
  36.5 0.0 copy-done.1
  36.5 0.0 copy-done.2
  36.5 2.0 %fusion.5 = bf16[64,8,256]{2,1,0:T(8,128)(2,1)} fusion(f32[512,512]{1,0:T(8,128)S(1)} %copy-done.1, f32[512,512]{1,0:T(8,128)S(1)} %copy-done.2, f32[512]{0:T(512)S(1)} %pad_maximum_fusion.4, f32[512]{0:T(512)S(1)} %pad_maximum_fusion.3, f32[256,256]{1,0:T(8,128)S(1)} %neg.6, f32[256,256]{1,0:T(8,128)S(1)} %reduce_sum.62, ...), kind=kOutput, calls=%fused_computation.12 | convolution fusion | flops 135921664 | bytes 3149824 | tf_op jit(solution)/shard_map/dot_general | solution.py:83
  38.5 0.0 copy-done.8
  38.5 9.5 %all-to-all-start.1 = ((bf16[64,8,256]{2,1,0:T(8,128)(2,1)}), bf16[64,8,256]{2,1,0:T(8,128)(2,1)S(1)}, u32[]{:S(2)}, u32[]{:S(2)}) async-start(bf16[64,8,256]{2,1,0:T(8,128)(2,1)} %fusion.5), calls=%async_computation.1 | async-start | bytes 524288 | tf_op jit(solution)/shard_map/all_to_all | solution.py:84
  48.1 0.1 mul.360
  48.2 0.6 eq.66
  48.8 0.1 eq.62
  48.9 0.6 reshape.283
  49.5 0.6 add.167
  50.1 0.8 fusion.47
  51.0 9.0 %all-to-all-done.1 = bf16[64,8,256]{2,1,0:T(8,128)(2,1)S(1)} async-done(((bf16[64,8,256]{2,1,0:T(8,128)(2,1)}), bf16[64,8,256]{2,1,0:T(8,128)(2,1)S(1)}, u32[]{:S(2)}, u32[]{:S(2)}) %all-to-all-start.1) | async-done | bytes 262176 | tf_op jit(solution)/shard_map/all_to_all | solution.py:84
  59.9 0.0 copy-done.10
  60.0 0.7 stack.3
  60.7 12.1 %all-to-all-start.2 = ((bf16[4,128,256]{2,1,0:T(8,128)(2,1)}), bf16[4,128,256]{2,1,0:T(8,128)(2,1)S(1)}, u32[]{:S(2)}, u32[]{:S(2)}) async-start(bf16[4,128,256]{2,1,0:T(8,128)(2,1)} %stack.3), calls=%async_computation.2 | async-start | bytes 524288 | tf_op jit(solution)/shard_map/all_to_all | solution.py:88
  72.8 0.9 fusion.36
  73.8 1.7 %fusion.8 = bf16[128,512]{1,0:T(8,128)(2,1)} fusion(bf16[64,512]{1,0:T(8,128)(2,1)} %constant.128.clone, s32[512]{0:T(512)S(1)} %add_select_fusion.3, s32[128]{0:T(128)} %copy-done.10, s32[128]{0:T(128)} %eq.66), kind=kOutput, calls=%fused_computation.18 | convolution fusion | flops 8593408 | bytes 199680 | tf_op jit(solution)/shard_map/dot_general | solution.py:102
  75.5 1.7 %fusion.7 = bf16[128,512]{1,0:T(8,128)(2,1)} fusion(bf16[64,512]{1,0:T(8,128)(2,1)} %constant.127.clone, s32[512]{0:T(512)S(1)} %add_select_fusion.3, s32[128]{0:T(128)} %copy-done.10, s32[128]{0:T(128)} %eq.66), kind=kOutput, calls=%fused_computation.17 | convolution fusion | flops 8593408 | bytes 199680 | tf_op jit(solution)/shard_map/dot_general | solution.py:102
  77.2 11.6 %all-to-all-done.2 = bf16[4,128,256]{2,1,0:T(8,128)(2,1)S(1)} async-done(((bf16[4,128,256]{2,1,0:T(8,128)(2,1)}), bf16[4,128,256]{2,1,0:T(8,128)(2,1)S(1)}, u32[]{:S(2)}, u32[]{:S(2)}) %all-to-all-start.2) | async-done | bytes 262176 | tf_op jit(solution)/shard_map/all_to_all | solution.py:88
  88.9 1.2 fusion.17
  90.1 1.4 fusion.26
  91.5 1.8 %fusion.75 = f32[128,512]{1,0:T(8,128)} fusion(bf16[128,256]{1,0:T(8,128)(2,1)S(1)} %get-tuple-element.16, bf16[256,512]{1,0:T(8,128)(2,1)} %constant.132), kind=kOutput, calls=%fused_computation.132 | convolution fusion | flops 33554432 | bytes 589824 | tf_op jit(solution)/shard_map/dot_general | solution.py:117
  93.3 1.6 %fusion.10 = f32[128,512]{1,0:T(8,128)S(1)} fusion(bf16[512,512]{1,0:T(8,128)(2,1)} %constant.129.clone, f32[128,512]{1,0:T(8,128)} %fusion.75, bf16[128,256]{1,0:T(8,128)(2,1)} %get-tuple-element.15, bf16[256,512]{1,0:T(8,128)(2,1)} %constant.133, f32[128,256]{1,0:T(8,128)S(1)} %fusion.36), kind=kOutput, calls=%fused_computation.20 | convolution fusion | flops 100925440 | bytes 1507328 | tf_op jit(solution)/shard_map/dot_general | solution.py:124
  95.0 0.8 fusion.28
  95.8 1.0 fusion.11
  96.8 17.1 %all_to_all.38 = bf16[64,8,256]{2,1,0:T(8,128)(2,1)S(1)} all-to-all(bf16[64,8,256]{2,1,0:T(8,128)(2,1)S(1)} %bitcast.125), channel_id=1, replica_groups=mesh['zl'=4,'y'=4,'core'=2,'zh'=4,'x'=4] {'zl','y','x'}, dimensions={0} | all-to-all | bytes 524288 | tf_op jit(solution)/shard_map/all_to_all | solution.py:136
  113.9 1.1 bitcast_convert_fusion.1
  115.1 7.3 %collective-permute-start.1 = (bf16[512,256]{1,0:T(8,128)(2,1)S(1)}, bf16[512,256]{1,0:T(8,128)(2,1)S(1)}, u32[]{:S(2)}, u32[]{:S(2)}) collective-permute-start(bf16[512,256]{1,0:T(8,128)(2,1)S(1)} %get-tuple-element.26), channel_id=1, source_target_pairs={{0,16},{16,0},{1,17},{17,1},{2,18},{18,2},{3,19},{19,3},{4,20},{20... | collective-permute-start | bytes 786440 | tf_op jit(solution)/shard_map/ppermute | solution.py:142
  122.4 1.1 collective-permute-done.1
  123.6 0.0 copy-start.4
  123.6 0.0 copy-start.6
  123.8 0.5 copy-done.4
  124.3 0.0 copy-done.6
  124.3 1.2 add_convert_fusion
  125.5 17.2 %all_to_all.39 = bf16[4,512,256]{2,1,0:T(8,128)(2,1)S(1)} all-to-all(bf16[4,512,256]{2,1,0:T(8,128)(2,1)S(1)} %add_convert_fusion), channel_id=1, replica_groups=mesh['zl'=4,'y'=4,'core'=2,'zh'=4,'x'=4] {'y'}, dimensions={0} | all-to-all | bytes 2097152 | tf_op jit(solution)/shard_map/all_to_all | solution.py:151
  142.8 1.3 copy.17
  144.1 1.5 %convert_element_type.115 = f32[4,512,256]{1,2,0:T(8,128)S(1)} convert(bf16[4,512,256]{1,2,0:T(8,128)(2,1)} %copy.17) | non-fusion elementwise | flops 524288 | bytes 3145728 | tf_op jit(solution)/shard_map/convert_element_type | solution.py:151
  145.6 1.8 %copy.18 = f32[512,1024]{1,0:T(8,128)} copy(f32[512,1024]{0,1:T(8,128)S(1)} %bitcast.113) | data formatting | bytes 4194304 | tf_op jit(solution)/shard_map/convert_element_type | solution.py:151
  (33 shorter events, 0.4 us)
Async XLA Ops:
  0.0 48.9 %copy-start = (bf16[8,256,256]{2,1,0:T(8,128)(2,1)S(1)}, bf16[8,256,256]{2,1,0:T(8,128)(2,1)}, u32[]{:S(2)}) copy-start(bf16[8,256,256]{2,1,0:T(8,128)(2,1)} %param.11) | copy-start | bytes 3145732
  1.6 6.3 %copy-start.9 = (s32[2]{0:T(128)S(1)}, s32[2]{0:T(128)}, u32[]{:S(2)}) copy-start(s32[2]{0:T(128)} %param.12) | copy-start | bytes 28
  2.9 14.8 %all-to-all-start = ((bf16[512,4,256]{2,0,1:T(8,128)(2,1)}), bf16[512,4,256]{2,0,1:T(8,128)(2,1)S(1)}, u32[]{:S(2)}, u32[]{:S(2)}) async-start(bf16[512,4,256]{2,0,1:T(8,128)(2,1)} %copy.16), calls=%async_computation | async-start | bytes 2097152 | tf_op jit(solution)/shard_map/all_to_all | solution.py:72
  10.1 10.3 %copy-start.3 = (f32[1,4,2,256]{3,1,2,0:T(4,128)}, f32[1,4,2,256]{3,1,2,0:T(4,128)S(1)}, u32[]{:S(2)}) copy-start(f32[1,4,2,256]{3,1,2,0:T(4,128)S(1)} %copy.22) | copy-start | bytes 24580
  10.1 10.2 %copy-start.5 = (f32[1,4,2,256]{3,1,2,0:T(4,128)}, f32[1,4,2,256]{3,1,2,0:T(4,128)S(1)}, u32[]{:S(2)}) copy-start(f32[1,4,2,256]{3,1,2,0:T(4,128)S(1)} %copy.21) | copy-start | bytes 24580
  20.4 16.2 %copy-start.1 = (f32[512,512]{1,0:T(8,128)S(1)}, f32[512,512]{1,0:T(8,128)}, u32[]{:S(2)}) copy-start(f32[512,512]{1,0:T(8,128)} %constant.131) | copy-start | bytes 3145732
  20.4 16.2 %copy-start.2 = (f32[512,512]{1,0:T(8,128)S(1)}, f32[512,512]{1,0:T(8,128)}, u32[]{:S(2)}) copy-start(f32[512,512]{1,0:T(8,128)} %constant.130) | copy-start | bytes 3145732
  23.5 13.1 %collective-permute-start = (bf16[512,256]{1,0:T(8,128)(2,1)}, bf16[512,256]{1,0:T(8,128)(2,1)}, u32[]{:S(2)}, u32[]{:S(2)}) collective-permute-start(bf16[512,256]{1,0:T(8,128)(2,1)} %pad_maximum_fusion.2), channel_id=1, source_target_pairs={{0,16},{16,0},{1,17},{17,1},{2,18},{18,2},{3,19},{19,3},{4,20},{20... | collective-permute-start | bytes 786440 | tf_op jit(solution)/shard_map/ppermute | solution.py:81
  32.6 6.0 %copy-start.7 = (f32[512]{0:T(512)}, f32[512]{0:T(512)S(1)}, u32[]{:S(2)}) copy-start(f32[512]{0:T(512)S(1)} %pad_maximum_fusion.4) | copy-start | bytes 6148
  32.6 5.9 %copy-start.8 = (f32[512]{0:T(512)}, f32[512]{0:T(512)S(1)}, u32[]{:S(2)}) copy-start(f32[512]{0:T(512)S(1)} %pad_maximum_fusion.3) | copy-start | bytes 6148
  35.5 12.6 %copy-start.11 = (s32[2,32]{1,0:T(2,128)S(1)}, s32[2,32]{1,0:T(2,128)}, u32[]{:S(2)}) copy-start(s32[2,32]{1,0:T(2,128)} %param.13) | copy-start | bytes 772
  35.5 12.6 %copy-start.12 = (s32[2,32]{1,0:T(2,128)S(1)}, s32[2,32]{1,0:T(2,128)}, u32[]{:S(2)}) copy-start(s32[2,32]{1,0:T(2,128)} %param.14) | copy-start | bytes 772
  38.5 21.4 %all-to-all-start.1 = ((bf16[64,8,256]{2,1,0:T(8,128)(2,1)}), bf16[64,8,256]{2,1,0:T(8,128)(2,1)S(1)}, u32[]{:S(2)}, u32[]{:S(2)}) async-start(bf16[64,8,256]{2,1,0:T(8,128)(2,1)} %fusion.5), calls=%async_computation.1 | async-start | bytes 524288 | tf_op jit(solution)/shard_map/all_to_all | solution.py:84
  48.9 11.0 %copy-start.10 = (s32[128]{0:T(128)}, s32[128]{0:T(128)S(1)}, u32[]{:S(2)}) copy-start(s32[128]{0:T(128)S(1)} %eq.62) | copy-start | bytes 1540
  60.7 28.2 %all-to-all-start.2 = ((bf16[4,128,256]{2,1,0:T(8,128)(2,1)}), bf16[4,128,256]{2,1,0:T(8,128)(2,1)S(1)}, u32[]{:S(2)}, u32[]{:S(2)}) async-start(bf16[4,128,256]{2,1,0:T(8,128)(2,1)} %stack.3), calls=%async_computation.2 | async-start | bytes 524288 | tf_op jit(solution)/shard_map/all_to_all | solution.py:88
  115.1 8.5 %collective-permute-start.1 = (bf16[512,256]{1,0:T(8,128)(2,1)S(1)}, bf16[512,256]{1,0:T(8,128)(2,1)S(1)}, u32[]{:S(2)}, u32[]{:S(2)}) collective-permute-start(bf16[512,256]{1,0:T(8,128)(2,1)S(1)} %get-tuple-element.26), channel_id=1, source_target_pairs={{0,16},{16,0},{1,17},{17,1},{2,18},{18,2},{3,19},{19,3},{4,20},{20... | collective-permute-start | bytes 786440 | tf_op jit(solution)/shard_map/ppermute | solution.py:142
  123.6 0.7 copy-start.4
  123.6 0.7 copy-start.6
